TPU v7x, 512 devices: a whole 4x8x8 slice. The times are simulated.
512 devices in a mesh: rows: 32 (over z, x), cols: 16 (over y, core).
Axes of the slice: x: 4, y: 8, z: 8, core: 2. Of those that a mesh axis runs over, the one named last changes fastest.
Arguments:
- row_features: float32 [16384, 64], P('rows'), may hold values from -6 to 6, as said below
- col_features: float32 [65536, 64], P('cols'), may hold values from -6 to 6, as said below
- test_block: bfloat16 [65536, 256], P('cols'), may hold values from -0.0234375 to 0.0234375, as said below
Outputs:
- basis: float32 [16384, 256], P('rows', 'cols')
- projected: float32 [256, 65536], P('rows', 'cols')
Inputs may be any that keep to these rules, and one draw needn't show every extreme that they name: `row_features`: independent entries of mean zero and unit variance. `col_features`: independent entries of mean zero and unit variance. `test_block`: independent entries of mean zero and variance 1 / 65536.
All inputs are finite; a program needn't handle non-finite values.
Results may differ from a plain program's by a relative error of at most 0.0095.
Values may be sent and summed in bfloat16 or wider, within the bound.
A program may use at most 64 MiB of HBM per device.

v0:
```python
import math

import jax
import jax.numpy as jnp
from jax import lax
from jax.sharding import Mesh
from jax.sharding import PartitionSpec as P

COLS = ("cols_0", "cols_1")


def split_up(x, dim, length):
    before, after = (x.shape[:dim], x.shape[dim + 1 :])
    return jnp.moveaxis(x.reshape(*before, length, -1, *after), dim, 0)


def summed_on_arrival(x, axis, dim):
    tiles = split_up(x, dim, lax.axis_size(axis))
    arrived = lax.all_to_all(tiles, axis, split_axis=0, concat_axis=0, tiled=True)
    return arrived.sum(axis=0)


def summed_rows(x, axes, dim):
    far, near = axes
    tiles = split_up(x, dim, lax.axis_size(far))
    nearer = summed_on_arrival(tiles, near, dim + 1)
    arrived = lax.all_to_all(nearer, far, split_axis=0, concat_axis=0, tiled=True)
    return arrived.sum(axis=0)


def filled_up(lines, length):
    spare = -lines.shape[0] % length
    if not spare:
        return lines
    return jnp.concatenate([lines, jnp.zeros((spare, *lines.shape[1:]), lines.dtype)])


def copy_for_each(x, axis):
    length = lax.axis_size(axis)
    return lax.all_to_all(jnp.broadcast_to(x[None], (length, *x.shape)), axis, 0, 0, tiled=True)


def joined_along(tiles, dim):
    tiles = jnp.moveaxis(tiles, 0, dim)
    shape = tiles.shape
    return tiles.reshape(*shape[:dim], shape[dim] * shape[dim + 1], *shape[dim + 2 :])


def gather_axes(x, axes, dim):
    far, near = axes
    tiles = copy_for_each(copy_for_each(x, far), near)
    return joined_along(tiles.swapaxes(0, 1).reshape(-1, *x.shape), dim)


def sum_by_parts(x, axes):
    lines = x.reshape(-1, x.shape[-1])
    own = summed_rows(filled_up(lines, lax.axis_size(axes[0]) * lax.axis_size(axes[1])), axes, 0)
    whole = gather_axes(own, axes, 0)
    return whole[: len(lines)].reshape(x.shape)


def gather_directly(x, axis, dim):
    tiles = copy_for_each(x, axis)
    return joined_along(tiles, dim)


def total_of(x, axes):
    lines = x.reshape(-1, x.shape[-1])
    own = summed_on_arrival(filled_up(lines, lax.axis_size(axes)), axes, 0)
    whole = gather_directly(own, axes, 0)
    return whole[: len(lines)].reshape(x.shape)


def summed_on_arrival_2(x, axis, dim):
    length = lax.axis_size(axis)
    tiles = lax.all_to_all(split_up(x, dim, length), axis, 0, 0, tiled=True)
    return jnp.sum(tiles.astype(jnp.float32), axis=0)


def kernel_tile(rows, cols):
    width = rows.shape[1]
    inner = lax.dot_general(
        rows,
        cols,
        (((1,), (1,)), ((), ())),
        precision=lax.Precision.HIGHEST,
        preferred_element_type=jnp.float32,
    ) * (1.0 / math.sqrt(width))
    shifted = inner + 1.0
    return (shifted * shifted * shifted).astype(jnp.bfloat16)


def gram_of(values):
    return lax.dot_general(
        values,
        values,
        (((0,), (0,)), ((), ())),
        precision=lax.Precision.HIGHEST,
        preferred_element_type=jnp.float32,
    )


def local(row_features, col_features, test_block):
    tile = kernel_tile(row_features, col_features)
    partial_sketch = jnp.dot(tile, test_block, preferred_element_type=jnp.float32)
    columns = partial_sketch.shape[1]
    own_width = columns // lax.axis_size(COLS)
    sketch = sum_by_parts(partial_sketch, ("cols_0", "cols_1"))
    gram = total_of(gram_of(sketch), "rows")
    lower = jnp.linalg.cholesky(gram)
    basis_full = jax.scipy.linalg.solve_triangular(lower, sketch.T, lower=True).T
    basis = lax.dynamic_slice_in_dim(basis_full, lax.axis_index(COLS) * own_width, own_width, 1)
    basis_b = basis_full.astype(jnp.bfloat16)
    projected = summed_on_arrival_2(
        lax.dot_general(
            basis_b, tile, (((0,), (0,)), ((), ())), preferred_element_type=jnp.float32
        ).astype(jnp.bfloat16),
        "rows",
        0,
    )
    return (basis, projected)


def solution(mesh):
    split = Mesh(mesh.devices.reshape(mesh.shape["rows"], 8, 2), ("rows", "cols_0", "cols_1"))
    return jax.shard_map(
        local,
        mesh=split,
        in_specs=(P("rows", None), P(COLS, None), P(COLS, None)),
        out_specs=(P("rows", COLS), P("rows", COLS)),
        check_vma=False,
    )
```

profile of v0, /device:TPU:1, one launch (start us, length us, event | category | flops | bytes accessed | tf_op | source)
XLA Modules:
  0.0 215.0 jit_solution(6264502264465524781)
XLA Ops:
  0.6 9.1 %fusion = bf16[512,4096]{1,0:T(8,128)(2,1)S(1)} fusion(f32[512,64]{0,1:T(8,128)} %param.3, f32[4096,64]{0,1:T(8,128)} %param.4), kind=kOutput, calls=%fused_computation.3 | convolution fusion | flops 1621098496 | bytes 5373952 | tf_op jit(solution)/shard_map/dot_general | solution.py:82
  9.8 1.3 fusion.18
  11.7 10.6 %all_to_all.35 = f32[2,8,32,256]{3,2,1,0:T(8,128)S(1)} all-to-all(f32[2,8,32,256]{3,2,1,0:T(8,128)S(1)} %bitcast.61), channel_id=1, replica_groups=mesh['rows'=32,'cols_0'=8,'cols_1'=2] {'cols_1'}, dimensions={0} | all-to-all | bytes 1048576 | tf_op jit(solution)/shard_map/all_to_all | solution.py:19
  22.3 14.7 %all_to_all.36 = f32[8,32,256]{2,1,0:T(8,128)S(1)} all-to-all(f32[8,32,256]{2,1,0:T(8,128)S(1)} %reduce_sum.36), channel_id=1, replica_groups=mesh['rows'=32,'cols_0'=8,'cols_1'=2] {'cols_0'}, dimensions={0} | all-to-all | bytes 524288 | tf_op jit(solution)/shard_map/all_to_all | solution.py:27
  37.1 14.2 %all_to_all.37 = f32[8,32,256]{2,1,0:T(8,128)S(1)} all-to-all(f32[8,32,256]{2,1,0:T(8,128)S(1)} %broadcast_in_dim.7), channel_id=1, replica_groups=mesh['rows'=32,'cols_0'=8,'cols_1'=2] {'cols_0'}, dimensions={0} | all-to-all | bytes 524288 | tf_op jit(solution)/shard_map/all_to_all | solution.py:40
  51.4 4.8 %all_to_all.38 = f32[2,8,32,256]{3,2,1,0:T(8,128)S(1)} all-to-all(f32[2,8,32,256]{3,2,1,0:T(8,128)S(1)} %broadcast_in_dim.8), channel_id=1, replica_groups=mesh['rows'=32,'cols_0'=8,'cols_1'=2] {'cols_1'}, dimensions={0} | all-to-all | bytes 1048576 | tf_op jit(solution)/shard_map/all_to_all | solution.py:40
  56.4 0.6 fusion.3
  57.0 21.9 %all_to_all.39 = f32[32,8,256]{2,1,0:T(8,128)S(1)} all-to-all(f32[32,8,256]{2,1,0:T(8,128)S(1)} %fusion.3), channel_id=1, replica_groups=mesh['rows'=32,'cols_0'=8,'cols_1'=2] {'rows'}, dimensions={0} | all-to-all | bytes 524288 | tf_op jit(solution)/shard_map/all_to_all | solution.py:19
  79.0 0.7 broadcast_in_dim.9
  79.7 4.8 %all-to-all-start.5 = ((f32[32,8,256]{2,1,0:T(8,128)}), f32[32,8,256]{2,1,0:T(8,128)S(1)}, u32[]{:S(2)}, u32[]{:S(2)}) async-start(f32[32,8,256]{2,1,0:T(8,128)} %broadcast_in_dim.9), calls=%async_computation.5 | async-start | bytes 524288 | tf_op jit(solution)/shard_map/all_to_all | solution.py:40
  84.5 10.4 %all-to-all-done.5 = f32[32,8,256]{2,1,0:T(8,128)S(1)} async-done(((f32[32,8,256]{2,1,0:T(8,128)}), f32[32,8,256]{2,1,0:T(8,128)S(1)}, u32[]{:S(2)}, u32[]{:S(2)}) %all-to-all-start.5) | async-done | bytes 262176 | tf_op jit(solution)/shard_map/all_to_all | solution.py:40
  95.2 11.7 %cholesky.50 = f32[128,128]{1,0:T(8,128)S(1)} custom-call(f32[128,128]{1,0:T(8,128)S(1)} %cholesky.118), custom_call_target="Cholesky" | custom-call | tf_op jit(solution)/shard_map/jit(cholesky)/cholesky | solution.py:110
  106.9 9.8 %custom-call.15 = f32[1,128,128]{1,2,0:T(8,128)S(1)} custom-call(f32[1,128,128]{2,1,0:T(8,128)S(1)} %get-tuple-element.23), custom_call_target="InvertDiagBlocksLowerTriangular" | custom-call | tf_op jit(solution)/shard_map/jit(cholesky)/cholesky | solution.py:110
  117.2 11.7 %cholesky.105 = f32[128,128]{1,0:T(8,128)S(1)} custom-call(f32[128,128]{1,0:T(8,128)S(1)} %convolution_subtract_fusion.1), custom_call_target="Cholesky" | custom-call | tf_op jit(solution)/shard_map/jit(cholesky)/cholesky | solution.py:110
  129.0 0.7 compare_reduce_fusion
  131.0 3.9 %while.1 = (s32[]{:T(128)}, f32[256,256]{1,0:T(8,128)S(1)}, s32[2,2]{1,0:T(2,128)S(1)}, f32[2,128,128]{2,1,0:T(8,128)S(1)}, s32[]{:T(128)}) while((s32[]{:T(128)}, f32[256,256]{1,0:T(8,128)S(1)}, s32[2,2]{1,0:T(2,128)S(1)}, f32[2,128,128]{2,1,0:T(8,128)S(1)}, s32[]{:T(128)}) %tuple.27), condition=%wide.while_cond, body=%wide.while_body.sunk | while | flops 2 | bytes 131181 | solution.py:111
  131.6 1.4 bitcast_dynamic-update-slice_fusion.2
  133.6 1.4 bitcast_dynamic-update-slice_fusion.2
  134.9 19.9 %custom-call.16 = f32[2,128,128]{1,2,0:T(8,128)S(1)} custom-call(f32[2,128,128]{2,1,0:T(8,128)S(1)} %get-tuple-element.9), custom_call_target="InvertDiagBlocksLowerTriangular" | custom-call | tf_op jit(solution)/shard_map/jit(_solve_triangular)/triangular_solve | solution.py:111
  156.3 4.8 %fusion.1 = bf16[32,8,4096]{2,1,0:T(8,128)(2,1)} fusion(bf16[512,4096]{1,0:T(8,128)(2,1)} %copy-done.1, f32[128,512]{1,0:T(8,128)S(1)} %fusion.10, f32[128,512]{1,0:T(8,128)S(1)} %fusion.6), kind=kOutput, calls=%fused_computation.5 | convolution fusion | flops 1075314688 | bytes 6815744 | tf_op jit(solution)/shard_map/dot_general | solution.py:115
  161.1 5.3 %all-to-all-start.6 = ((bf16[32,8,4096]{2,1,0:T(8,128)(2,1)}), bf16[32,8,4096]{2,1,0:T(8,128)(2,1)}, u32[]{:S(2)}, u32[]{:S(2)}) async-start(bf16[32,8,4096]{2,1,0:T(8,128)(2,1)} %fusion.1), calls=%async_computation.6 | async-start | bytes 4194304 | tf_op jit(solution)/shard_map/all_to_all | solution.py:76
  166.4 0.6 fusion.15
  167.0 45.4 %all-to-all-done.6 = bf16[32,8,4096]{2,1,0:T(8,128)(2,1)} async-done(((bf16[32,8,4096]{2,1,0:T(8,128)(2,1)}), bf16[32,8,4096]{2,1,0:T(8,128)(2,1)}, u32[]{:S(2)}, u32[]{:S(2)}) %all-to-all-start.6) | async-done | bytes 2097184 | tf_op jit(solution)/shard_map/all_to_all | solution.py:76
  212.4 2.5 %convert_reduce_fusion = f32[8,4096]{1,0:T(8,128)} fusion(bf16[32,8,4096]{2,1,0:T(8,128)(2,1)} %all-to-all-done.6), kind=kLoop, calls=%fused_computation.6 | loop fusion | flops 2064384 | bytes 2228224 | tf_op jit(solution)/shard_map/reduce_sum | solution.py:77
  (31 shorter events, 4.4 us)
Async XLA Ops:
  0.6 9.1 %copy-start = (bf16[4096,256]{1,0:T(8,128)(2,1)S(1)}, bf16[4096,256]{1,0:T(8,128)(2,1)}, u32[]{:S(2)}) copy-start(bf16[4096,256]{1,0:T(8,128)(2,1)} %param.5) | copy-start | bytes 6291460
  9.8 1.9 copy-start.1
  79.7 15.3 %all-to-all-start.5 = ((f32[32,8,256]{2,1,0:T(8,128)}), f32[32,8,256]{2,1,0:T(8,128)S(1)}, u32[]{:S(2)}, u32[]{:S(2)}) async-start(f32[32,8,256]{2,1,0:T(8,128)} %broadcast_in_dim.9), calls=%async_computation.5 | async-start | bytes 524288 | tf_op jit(solution)/shard_map/all_to_all | solution.py:40
  161.1 51.4 %all-to-all-start.6 = ((bf16[32,8,4096]{2,1,0:T(8,128)(2,1)}), bf16[32,8,4096]{2,1,0:T(8,128)(2,1)}, u32[]{:S(2)}, u32[]{:S(2)}) async-start(bf16[32,8,4096]{2,1,0:T(8,128)(2,1)} %fusion.1), calls=%async_computation.6 | async-start | bytes 4194304 | tf_op jit(solution)/shard_map/all_to_all | solution.py:76
where the time goes:
time: 219 us; the launch traced here: 215 us
  blocking collectives  66.3 us (30%)
  other arithmetic  57.2 us (26%)
  waiting for transfers between devices  55.9 us (26%)
  matrix products  17.7 us (8%)
  starting transfers between devices  10.1 us (5%)
  local copies, waits for them, and re-layouts  5.74 us (3%)
    all_to_all x1, waiting for transfers between devices, summed_on_arrival_2(): tiles = lax.all_to_all(split_up(x, dim, length), axis, 0, 0, tiled=True)  45.4 us
    another operation x6, other arithmetic, local(): lower = jnp.linalg.cholesky(gram)  34 us
    all_to_all x2, blocking collectives, summed_on_arrival(): lax.all_to_all(tiles, axis, split_axis=0, concat_axis=0, tiled=True)  32.5 us
    another operation x3, other arithmetic, local(): jax.scipy.linalg.solve_triangular(lower, sketch.T, lower=True)  19.9 us
    all_to_all x2, blocking collectives, copy_for_each(): lax.all_to_all(jnp.broadcast_to(x[None], (length, *x.shape)), axis, 0, 0,...  19 us
    all_to_all x1, blocking collectives, summed_rows(): lax.all_to_all(nearer, far, split_axis=0, concat_axis=0, tiled=True)  14.7 us
    all_to_all x1, waiting for transfers between devices, copy_for_each(): lax.all_to_all(jnp.broadcast_to(x[None], (length, *x.shape)), axis, 0, 0,...  10.4 us
    dot_general x1, matrix products, kernel_tile(): lax.dot_general(rows, cols, (((1,), (1,)), ((), ())), precision=lax.Preci...  9.12 us
  transfers between devices with their start and end apart: 2, of which 2 were waited for; matrix products, arithmetic and copies ran while one was open for 0% of the time, Pallas kernels for 0%

commit v1 on v0

v1 whole, which is shorter than its diff:
```python
import functools
import math

import jax
import jax.numpy as jnp
from jax import lax
from jax.experimental import pallas as pl
from jax.experimental.pallas import tpu as pltpu
from jax.sharding import PartitionSpec as P

MESH = pl.DeviceIdType.MESH
F32, BF16 = jnp.float32, jnp.bfloat16
ALONG_X = 4
PANEL = 16
CHUNK = 512


def far_first(length):
    return sorted(range(1, length), key=lambda i: -min(i, length - i))


def split2(v):
    high = v.astype(BF16)
    return high, (v - high.astype(F32)).astype(BF16)


def split3(v):
    high = v.astype(BF16)
    rest = v - high.astype(F32)
    mid = rest.astype(BF16)
    return high, mid, (rest - mid.astype(F32)).astype(BF16)


def dot(a, b, dims=((1,), (0,))):
    return lax.dot_general(a, b, (dims, ((), ())), preferred_element_type=F32)


def cubed(inner):
    shifted = inner + 1.0
    return (shifted * shifted * shifted).astype(BF16)


def left_terms(features_t, scale):
    high, low = split2(features_t * scale)
    return jnp.concatenate([high, high, low], axis=0).T


def right_terms(features_t, scale):
    high, low = split2(features_t * scale)
    return jnp.concatenate([high, low, high], axis=0)


def eliminate(work):
    n = work.shape[0]
    row = lax.broadcasted_iota(jnp.int32, (PANEL, 1), 0)
    for p in range(n // PANEL):
        first = p * PANEL
        base = (first // 128) * 128
        offset = first - base
        end = n + ((first + PANEL + 127) // 128) * 128
        panel = work[first : first + PANEL, base:end]
        tiles = panel.shape[1] // 128
        column = [
            jnp.broadcast_to(panel[:, offset + j : offset + j + 1], (PANEL, 128))
            for j in range(PANEL)
        ]
        for k in range(PANEL):
            inverse_root = lax.rsqrt(column[k][k : k + 1, :])
            lower = column[k] * inverse_root
            for j in range(k + 1, PANEL):
                column[j] = column[j] - lower * lower[j : j + 1, :]
            pivot_row = panel[k : k + 1, :] * jnp.concatenate([inverse_root] * tiles, axis=1)
            below = jnp.concatenate([jnp.where(row > k, lower, 0.0)] * tiles, axis=1)
            panel = jnp.where(
                row == k, jnp.broadcast_to(pivot_row, panel.shape), panel - below * pivot_row
            )
        work[first : first + PANEL, base:end] = panel
        after = first + PANEL
        if after < n:
            high, mid, low = split3(panel)
            start = (after // 128) * 128
            keep = slice(start - base, n - base)
            left = jnp.concatenate([t[:, keep] for t in (high, high, mid, high, mid, low)], axis=0)
            right = jnp.concatenate([high, mid, high, low, mid, high], axis=0)
            work[after:, base:end] = work[after:, base:end] - dot(left.T[after - start :, :], right)


def kernel(
    nx, nz, nc,
    row_ref, col_ref, test_ref, basis_ref, out_ref,
    row_left, col_left, partial, rs_send, rs_recv, rows_recv, own_sketch, sketch,
    tile_t, gram, gx_recv, gz_send, gz_recv, gy_send, gram_all,
    p_send, p_recv, work, o_send, o_recv,
    rows_sem, rs_sem, ag_sem, gx_sem, xag_sem, fwd_sem, gz_sem, gy_sem, p_sem, o_sem,
):
    r, c = lax.axis_index("rows"), lax.axis_index("cols")
    z, x = r // nx, lax.rem(r, nx)
    rows, size = partial.shape
    width = row_ref.shape[0]
    scale = 1.0 / math.sqrt(width)
    columns = col_ref.shape[1]
    per_x = columns // nx
    per_z = per_x // nz
    half = lax.rem(c, 2)

    def at_x(i):
        return (z * nx + lax.rem(x + i, nx), c)

    def at_z(i):
        return (lax.rem(z + i, nz) * nx + x, c)

    def at_c(i):
        return (r, lax.rem(c + i, nc))

    def at_zx(i, j):
        return (lax.rem(z + i, nz) * nx + lax.rem(x + j, nx), c)

    around = [(i, j) for i in range(nz) for j in range(nx) if (i, j) != (0, 0)]
    around.sort(key=lambda ij: -min(ij[0], nz - ij[0]) - min(ij[1], nx - ij[1]))

    def copy(src, dst, sems, k, device):
        return pltpu.make_async_remote_copy(
            src_ref=src,
            dst_ref=dst,
            send_sem=sems.at[0, k],
            recv_sem=sems.at[1, k],
            device_id=device,
            device_id_type=MESH,
        )

    barrier = pltpu.get_barrier_semaphore()
    for i in range(1, nc):
        pl.semaphore_signal(barrier, inc=1, device_id=at_c(i), device_id_type=MESH)
    for i, j in around:
        pl.semaphore_signal(barrier, inc=1, device_id=at_zx(i, j), device_id_type=MESH)

    row_left[...] = left_terms(row_ref[...], scale)
    partial[...] = jnp.zeros_like(partial)

    @pl.loop(0, columns // CHUNK)
    def _(n):
        at = pl.ds(pl.multiple_of(n * CHUNK, CHUNK), CHUNK)
        tile = cubed(dot(row_left[...], right_terms(col_ref[:, at], 1.0)))
        partial[...] += dot(tile, test_ref[at, :])

    rs_send[...] = partial[...].astype(BF16).reshape(rs_send.shape)

    pl.semaphore_wait(barrier, nc - 1 + len(around))

    piece = rows // nc
    rs = {i: copy(rs_send.at[lax.rem(c + i, nc)], rs_recv.at[i - 1], rs_sem, i - 1, at_c(i)) for i in far_first(nc)}
    for i in far_first(nc):
        rs[i].start()
    feat = [copy(row_ref, rows_recv.at[i - 1], rows_sem, i - 1, at_x(i)) for i in range(1, nx)]
    for one in feat:
        one.start()
    own = pl.ds(pl.multiple_of(x * per_x, per_x), per_x)
    col_left[...] = left_terms(col_ref[:, own], 1.0)
    total = partial[pl.ds(pl.multiple_of(c * piece, piece), piece), :]
    for i in range(1, nc):
        rs[i].wait_recv()
        total = total + rs_recv[i - 1].astype(F32)
    own_sketch[...] = total.astype(BF16)
    sketch[x, c] = own_sketch[...]

    ag = {i: copy(own_sketch, sketch.at[x, c], ag_sem, i - 1, at_c(i)) for i in far_first(nc)}
    for i in far_first(nc):
        ag[i].start()

    block = min(256, per_x)
    for i in range(nx):
        if i:
            feat[i - 1].wait_recv()
        source = rows_recv[i - 1] if i else row_ref[...]
        right = right_terms(source, scale)
        at_block = lax.rem(x + nx - i, nx)

        @pl.loop(0, per_x // block)
        def _(m):
            at = pl.ds(pl.multiple_of(m * block, block), block)
            tile_t[at_block, at, :] = cubed(dot(col_left[at, :], right))

    for i in range(1, nc):
        ag[i].wait_recv()

    held = sketch[x].reshape(rows, size)
    gram[...] = dot(held, held, ((0,), (0,))).reshape(gram.shape)
    gx = [copy(gram.at[c], gx_recv.at[i - 1], gx_sem, i - 1, at_x(i)) for i in range(1, nx)]
    for one in gx:
        one.start()
    mine = pl.ds(half * (nc // 2), nc // 2)
    xag = [
        copy(sketch.at[x, mine], sketch.at[x, mine], xag_sem, i - 1, at_x(i)) for i in range(1, nx)
    ]
    for one in xag:
        one.start()
    slice_sum = gram[c]
    for i in range(1, nx):
        gx[i - 1].wait_recv()
        slice_sum = slice_sum + gx_recv[i - 1]
    gz_send[...] = slice_sum
    gz = {i: copy(gz_send, gz_recv.at[i - 1], gz_sem, i - 1, at_z(i)) for i in far_first(nz)}
    for i in far_first(nz):
        gz[i].start()

    sibling = (r, c + 1 - 2 * half)
    fwd = []
    for i in range(1, nx):
        xag[i - 1].wait_recv()
        there = sketch.at[lax.rem(x + nx - i, nx), mine]
        fwd.append(copy(there, there, fwd_sem, i - 1, sibling))
        fwd[-1].start()

    for i in range(1, nz):
        gz[i].wait_recv()
        slice_sum = slice_sum + gz_recv[i - 1]
    gy_send[...] = slice_sum
    gram_all[c] = slice_sum
    gy = {i: copy(gy_send, gram_all.at[c], gy_sem, i - 1, at_c(i)) for i in far_first(nc)}
    for i in far_first(nc):
        gy[i].start()

    for i in range(1, nx):
        fwd[i - 1].wait_recv()
    block = min(2 * per_z, per_x)

    @pl.loop(0, per_x // block)
    def _(m):
        at = pl.ds(pl.multiple_of(m * block, block), block)
        total = dot(tile_t[0, at, :], sketch[0].reshape(rows, size))
        for i in range(1, nx):
            total = total + dot(tile_t[i, at, :], sketch[i].reshape(rows, size))
        count = block // per_z
        p_send[pl.ds(m * count, count)] = total.astype(BF16).reshape(count, per_z, size)

    ps = {i: copy(p_send.at[lax.rem(z + i, nz)], p_recv.at[i - 1], p_sem, i - 1, at_z(i)) for i in far_first(nz)}
    for i in far_first(nz):
        ps[i].start()

    for i in range(1, nc):
        gy[i].wait_recv()
    work[:, :size] = gram_all[...].reshape(size, size)
    diagonal = lax.broadcasted_iota(jnp.int32, (size, size), 0)
    work[:, size:] = jnp.where(diagonal == lax.broadcasted_iota(jnp.int32, (size, size), 1), 1.0, 0.0)
    eliminate(work)

    product = p_send[z].astype(F32)
    for i in range(1, nz):
        ps[i].wait_recv()
        product = product + p_recv[i - 1].astype(F32)
    inverse_high, inverse_low = split2(work[:, size:])
    product_high, product_low = split2(product)
    result = dot(
        jnp.concatenate([inverse_high, inverse_high, inverse_low], axis=1),
        jnp.concatenate([product_high, product_low, product_high], axis=1),
        ((1,), (1,)),
    )
    o_send[...] = result.reshape(o_send.shape)
    mine = pl.ds(pl.multiple_of(x * per_x + z * per_z, per_z), per_z)
    outs = []
    for k, (i, j) in enumerate(around):
        target = at_zx(i, j)
        outs.append(copy(o_send.at[target[0]], o_recv.at[:, mine], o_sem, k, target))
        outs[-1].start()
    o_recv[:, mine] = o_send[r]
    share = size // nc
    share_high, share_low = split2(work[pl.ds(pl.multiple_of(c * share, share), share), size:])
    held = sketch[x].reshape(rows, size)
    basis_ref[...] = dot(share_high, held, ((1,), (1,))) + dot(share_low, held, ((1,), (1,)))
    for one in outs:
        one.wait_recv()
    out_ref[...] = o_recv[...]

    for group in (feat, rs.values(), ag.values(), gx, xag, gz.values(), fwd, gy.values(), ps.values(), outs):
        for one in group:
            one.wait_send()


def local(nx, nz, nc, row_features, col_features, test_block):
    rows, width = row_features.shape
    columns, size = test_block.shape
    per_x = columns // nx
    per_z = per_x // nz
    share = size // nc
    piece = rows // nc
    vmem = pltpu.VMEM

    def sems(count):
        return pltpu.SemaphoreType.DMA((2, count))

    basis_t, projected = pl.pallas_call(
        functools.partial(kernel, nx, nz, nc),
        out_shape=(
            jax.ShapeDtypeStruct((share, rows), F32),
            jax.ShapeDtypeStruct((size // (nx * nz), columns), F32),
        ),
        in_specs=[pl.BlockSpec(memory_space=vmem)] * 3,
        out_specs=(pl.BlockSpec(memory_space=vmem),) * 2,
        scratch_shapes=[
            vmem((rows, 3 * width), BF16),
            vmem((per_x, 3 * width), BF16),
            vmem((rows, size), F32),
            vmem((nc, piece, size), BF16),
            vmem((nc - 1, piece, size), BF16),
            vmem((nx - 1, width, rows), F32),
            vmem((piece, size), BF16),
            vmem((nx, nc, piece, size), BF16),
            vmem((nx, per_x, rows), BF16),
            vmem((nc, share, size), F32),
            vmem((nx - 1, share, size), F32),
            vmem((share, size), F32),
            vmem((nz - 1, share, size), F32),
            vmem((share, size), F32),
            vmem((nc, share, size), F32),
            vmem((nz, per_z, size), BF16),
            vmem((nz - 1, per_z, size), BF16),
            vmem((size, 2 * size), F32),
            vmem((nx * nz, size // (nx * nz), per_z), F32),
            vmem((size // (nx * nz), columns), F32),
            sems(nx - 1),
            sems(nc - 1),
            sems(nc - 1),
            sems(nx - 1),
            sems(nx - 1),
            sems(nx - 1),
            sems(nz - 1),
            sems(nc - 1),
            sems(nz - 1),
            sems(nx * nz - 1),
        ],
        compiler_params=pltpu.CompilerParams(
            collective_id=0, has_side_effects=True, vmem_limit_bytes=56 * 1024 * 1024
        ),
    )(row_features.T, col_features.T, test_block)
    return basis_t.T, projected


def solution(mesh, nx=ALONG_X):
    nz, nc = mesh.shape["rows"] // nx, mesh.shape["cols"]
    return jax.shard_map(
        functools.partial(local, nx, nz, nc),
        mesh=mesh,
        in_specs=(P("rows", None), P("cols", None), P("cols", None)),
        out_specs=(P("rows", "cols"), P("rows", "cols")),
        check_vma=False,
    )
```

time: 219 us -> 71.8 us (0.33); the launches traced: 215 us -> 71.4 us
  Pallas kernels: 0 us -> 67.8 us
  blocking collectives: 66.3 us -> 0 us
  other arithmetic: 57.2 us -> 0 us
  waiting for transfers between devices: 55.9 us -> 0 us
  matrix products: 17.7 us -> 0 us
  starting transfers between devices: 10.1 us -> 0 us
  local copies, waits for them, and re-layouts: 5.74 us -> 2.94 us
    pallas_call x0 -> x1, Pallas kernels: none -> 67.8 us  [local(): pl.pallas_call(functools.partial(kernel, nx, nz, nc), out_shape=(jax.Shap...]
    all_to_all x5 -> x0, blocking collectives: 66.3 us -> none  [the longest x2 32.5 us: summed_on_arrival(): lax.all_to_all(tiles, axis, split_axis=0, concat_axis=0, tiled=True)]
    all_to_all x2 -> x0, waiting for transfers between devices: 55.9 us -> none  [the longest x1 45.4 us: summed_on_arrival_2(): tiles = lax.all_to_all(split_up(x, dim, length), axis, 0, 0, tiled=True)]
    another operation x9 -> x0, other arithmetic: 53.9 us -> none  [the longest x6 34 us: local(): lower = jnp.linalg.cholesky(gram)]
    dot_general x4 -> x0, matrix products: 15.8 us -> none  [the longest x1 9.12 us: kernel_tile(): lax.dot_general(rows, cols, (((1,), (1,)), ((), ())), precision=lax.Preci...]
    all_to_all x2 -> x0, starting transfers between devices: 10.1 us -> none  [the longest x1 5.33 us: summed_on_arrival_2(): tiles = lax.all_to_all(split_up(x, dim, length), axis, 0, 0, tiled=True)]
    another operation x10 -> x0, local copies, waits for them, and re-layouts: 4.03 us -> none
    reduce_sum x4 -> x0, other arithmetic: 2.63 us -> none  [the longest x1 2.54 us: summed_on_arrival_2(): return jnp.sum(tiles.astype(jnp.float32), axis=0)]
  transfers between devices with their start and end apart: 2 -> 0, of which waited for: 2 -> 0; matrix products, arithmetic and copies ran while one was open for 0% -> 0% of each run, Pallas kernels for 0% -> 0%
where the time goes in v1:
time: 71.8 us; the launch traced here: 71.4 us
  Pallas kernels  67.8 us (94%)
  local copies, waits for them, and re-layouts  2.94 us (4%)
    pallas_call x1, Pallas kernels, local(): pl.pallas_call(functools.partial(kernel, nx, nz, nc), out_shape=(jax.Shap...  67.8 us
    unnamed x2, local copies, waits for them, and re-layouts  2.94 us

profile of v1, /device:TPU:1, one launch (start us, length us, event | category | flops | bytes accessed | tf_op | source)
XLA Modules:
  0.0 71.4 jit_solution(5281789867044474498)
XLA Ops:
  0.6 67.8 %shard_map.50 = (f32[16,512]{1,0:T(8,128)}, f32[8,4096]{1,0:T(8,128)}) custom-call(f32[64,512]{1,0:T(8,128)} %bitcast.4, f32[64,4096]{1,0:T(8,128)} %bitcast.3, bf16[4096,256]{1,0:T(8,128)(2,1)} %test_ref.1), custom_call_target="tpu_custom_call" | custom-call | tf_op jit(solution)/shard_map/pallas_call | solution.py:291
  68.5 1.4 %copy.7 = f32[512,16]{0,1:T(8,128)} copy(f32[512,16]{0,1:T(8,128)} %bitcast.5) | data formatting | bytes 65536
  69.8 1.6 %copy.8 = f32[8,4096]{1,0:T(8,128)} copy(f32[8,4096]{1,0:T(8,128)} %get-tuple-element.9) | data formatting | bytes 262144

commit v2 on v1

v2 whole, which is shorter than its diff:
```python
import functools
import math

import jax
import jax.numpy as jnp
from jax import lax
from jax.experimental import pallas as pl
from jax.experimental.pallas import tpu as pltpu
from jax.sharding import PartitionSpec as P

MESH = pl.DeviceIdType.MESH
F32, BF16 = jnp.float32, jnp.bfloat16
ALONG_X = 4
PANEL = 16
STEPS = 2
VMEM_LIMIT = 56_300_000


def far_first(length):
    return sorted(range(1, length), key=lambda i: -min(i, length - i))


def split2(v):
    high = v.astype(BF16)
    return high, (v - high.astype(F32)).astype(BF16)


def split3(v):
    high = v.astype(BF16)
    rest = v - high.astype(F32)
    mid = rest.astype(BF16)
    return high, mid, (rest - mid.astype(F32)).astype(BF16)


def dot(a, b, dims=((1,), (0,))):
    return lax.dot_general(a, b, (dims, ((), ())), preferred_element_type=F32)


def cubed(inner):
    shifted = inner + 1.0
    return (shifted * shifted * shifted).astype(BF16)


def left_terms(features_t, scale):
    high, low = split2(features_t * scale)
    return jnp.concatenate([high, high, low], axis=0).T


def right_terms(features_t, scale):
    high, low = split2(features_t * scale)
    return jnp.concatenate([high, low, high], axis=0)


def eliminate(work):
    n = work.shape[0]
    row = lax.broadcasted_iota(jnp.int32, (PANEL, 1), 0)
    for p in range(n // PANEL):
        first = p * PANEL
        base = (first // 128) * 128
        offset = first - base
        end = n + ((first + PANEL + 127) // 128) * 128
        panel = work[first : first + PANEL, base:end]
        tiles = panel.shape[1] // 128
        column = [
            jnp.broadcast_to(panel[:, offset + j : offset + j + 1], (PANEL, 128))
            for j in range(PANEL)
        ]
        for k in range(PANEL):
            inverse_root = lax.rsqrt(column[k][k : k + 1, :])
            lower = column[k] * inverse_root
            for j in range(k + 1, PANEL):
                column[j] = column[j] - lower * lower[j : j + 1, :]
            pivot_row = panel[k : k + 1, :] * jnp.concatenate([inverse_root] * tiles, axis=1)
            below = jnp.concatenate([jnp.where(row > k, lower, 0.0)] * tiles, axis=1)
            panel = jnp.where(
                row == k, jnp.broadcast_to(pivot_row, panel.shape), panel - below * pivot_row
            )
        work[first : first + PANEL, base:end] = panel
        after = first + PANEL
        if after < n:
            high, mid, low = split3(panel)
            start = (after // 128) * 128
            keep = slice(start - base, n - base)
            left = jnp.concatenate([t[:, keep] for t in (high, high, mid, high, mid, low)], axis=0)
            right = jnp.concatenate([high, mid, high, low, mid, high], axis=0)
            work[after:, base:end] = work[after:, base:end] - dot(left.T[after - start :, :], right)


def kernel(
    nx, nz, nc,
    row_hbm, col_hbm, test_hbm, basis_ref, out_ref,
    row_ref, col_ref, test_ref,
    row_left, col_left, partial, pair_send, pair_recv, rs_send, rs_recv, rows_recv, own_sketch, sketch,
    tile_t, gram, gx_recv, gz_send, gz_recv, gy_send, gram_all,
    p_send, p_recv, work, o_send, o_recv,
    in_sem, sent_sem, rows_sem, pair_sem, rs_sem, ag_sem, ag2_sem, gx_sem, xag_sem, fwd_sem, gz_sem, gy_sem, gy2_sem,
    p_sem, o_sem,
):
    r, c = lax.axis_index("rows"), lax.axis_index("cols")
    z, x = r // nx, lax.rem(r, nx)
    ny = nc // 2
    y, half = c // 2, lax.rem(c, 2)
    rows, size = partial.shape
    piece = rows // nc
    width = row_ref.shape[0]
    scale = 1.0 / math.sqrt(width)
    columns = col_ref.shape[1]
    per_x = columns // nx
    per_z = per_x // nz
    place = half * ny + y

    def at_x(i):
        return (z * nx + lax.rem(x + i, nx), c)

    def at_z(i):
        return (lax.rem(z + i, nz) * nx + x, c)

    def at_y(i):
        return (r, lax.rem(y + i, ny) * 2 + half)

    def at_zx(i, j):
        return (lax.rem(z + i, nz) * nx + lax.rem(x + j, nx), c)

    sibling = (r, c + 1 - 2 * half)
    around = [(i, j) for i in range(nz) for j in range(nx) if (i, j) != (0, 0)]
    around.sort(key=lambda ij: -min(ij[0], nz - ij[0]) - min(ij[1], nx - ij[1]))

    def copy(group, src, dst, recv_sem, device):
        return pltpu.make_async_remote_copy(
            src_ref=src,
            dst_ref=dst,
            send_sem=sent_sem.at[group],
            recv_sem=recv_sem,
            device_id=device,
            device_id_type=MESH,
        )

    def wait_sent(group, whole):
        copy(group, whole, whole, in_sem.at[0], sibling).wait_send()

    steps = [slice(n, n + columns // STEPS) for n in range(0, columns, columns // STEPS)]
    pieces = [(row_hbm, row_ref)]
    for at in steps:
        pieces += [(col_hbm.at[:, at], col_ref.at[:, at]), (test_hbm.at[at, :], test_ref.at[at, :])]
    loads = [pltpu.make_async_copy(src, dst, in_sem.at[k]) for k, (src, dst) in enumerate(pieces)]
    for one in loads:
        one.start()
    barrier = pltpu.get_barrier_semaphore()
    pl.semaphore_signal(barrier, inc=1, device_id=sibling, device_id_type=MESH)
    for i in far_first(ny):
        pl.semaphore_signal(barrier, inc=1, device_id=at_y(i), device_id_type=MESH)
    for i, j in around:
        pl.semaphore_signal(barrier, inc=1, device_id=at_zx(i, j), device_id_type=MESH)

    loads[0].wait()
    row_left[...] = left_terms(row_ref[...], scale)
    for n, at in enumerate(steps):
        loads[2 * n + 1].wait()
        tile = cubed(dot(row_left[...], right_terms(col_ref[:, at], 1.0)))
        loads[2 * n + 2].wait()
        share = dot(tile, test_ref[at, :])
        partial[...] = partial[...] + share if n else share

    def half_of(which):
        return pl.ds(pl.multiple_of(which * (rows // 2), rows // 2), rows // 2)

    pair_send[...] = partial[half_of(1 - half), :].astype(BF16)
    pl.semaphore_wait(barrier, ny + len(around))

    pair = copy(0, pair_send, pair_recv, pair_sem.at[0], sibling)
    pair.start()
    feat = [copy(1, row_ref, rows_recv.at[i - 1], rows_sem.at[i - 1], at_x(i)) for i in range(1, nx)]
    for one in feat:
        one.start()
    pair.wait_recv()
    partial[half_of(half), :] += pair_recv[...].astype(F32)
    rs_send[...] = partial[half_of(half), :].astype(BF16).reshape(rs_send.shape)
    rs = [copy(2, rs_send.at[lax.rem(y + i, ny)], rs_recv.at[i - 1], rs_sem.at[0], at_y(i)) for i in far_first(ny)]
    for one in rs:
        one.start()
    own = pl.ds(pl.multiple_of(x * per_x, per_x), per_x)
    col_left[...] = left_terms(col_ref[:, own], 1.0)
    total = partial[pl.ds(pl.multiple_of(place * piece, piece), piece), :]
    copy(2, rs_recv, rs_recv, rs_sem.at[0], sibling).wait_recv()
    for i in range(1, ny):
        total = total + rs_recv[i - 1].astype(F32)
    own_sketch[...] = total.astype(BF16)
    sketch[x, place] = own_sketch[...]

    ag = {i: copy(3, own_sketch, sketch.at[x, place], ag_sem.at[i - 1], at_y(i)) for i in far_first(ny)}
    for i in far_first(ny):
        ag[i].start()
    copy(4, own_sketch, sketch.at[x, place], ag2_sem.at[0], sibling).start()

    block = min(256, per_x)
    for i in range(nx):
        if i:
            feat[i - 1].wait_recv()
        source = rows_recv[i - 1] if i else row_ref[...]
        right = right_terms(source, scale)
        at_block = lax.rem(x + nx - i, nx)

        @pl.loop(0, per_x // block)
        def _(m):
            at = pl.ds(pl.multiple_of(m * block, block), block)
            tile_t[at_block, at, :] = cubed(dot(col_left[at, :], right))

    near_first = far_first(ny)[::-1]
    for i in near_first:
        ag[i].wait_recv()
        there = sketch.at[x, half * ny + lax.rem(y + ny - i, ny)]
        copy(4, there, there, ag2_sem.at[0], sibling).start()
    mine = pl.ds(half * ny, ny)
    other = pl.ds((1 - half) * ny, ny)
    copy(4, sketch.at[x, other], sketch.at[x, other], ag2_sem.at[0], sibling).wait_recv()

    held = sketch[x].reshape(rows, size)
    whole = dot(held, held, ((0,), (0,)))
    top = size // 2
    part = top // nc
    gram[:, 0] = whole[:top, :top].reshape(nc, part, top)
    gram[:, 1] = whole[:top, top:].reshape(nc, part, top)
    gram[:, 2] = whole[top:, top:].reshape(nc, part, top)
    gx = [copy(5, gram.at[place], gx_recv.at[i - 1], gx_sem.at[0], at_x(i)) for i in range(1, nx)]
    for one in gx:
        one.start()
    xag = [copy(6, sketch.at[x, mine], sketch.at[x, mine], xag_sem.at[i - 1], at_x(i)) for i in range(1, nx)]
    for one in xag:
        one.start()
    slice_sum = gram[place]
    copy(5, gx_recv, gx_recv, gx_sem.at[0], sibling).wait_recv()
    for i in range(1, nx):
        slice_sum = slice_sum + gx_recv[i - 1]
    gz_send[...] = slice_sum
    gz = [copy(7, gz_send, gz_recv.at[i - 1], gz_sem.at[0], at_z(i)) for i in far_first(nz)]
    for one in gz:
        one.start()

    for i in range(1, nx):
        xag[i - 1].wait_recv()
        there = sketch.at[lax.rem(x + nx - i, nx), mine]
        copy(8, there, there, fwd_sem.at[i - 1], sibling).start()

    copy(7, gz_recv, gz_recv, gz_sem.at[0], sibling).wait_recv()
    for i in range(1, nz):
        slice_sum = slice_sum + gz_recv[i - 1]
    gy_send[...] = slice_sum
    gram_all[place] = slice_sum
    gy = {i: copy(9, gy_send, gram_all.at[place], gy_sem.at[i - 1], at_y(i)) for i in far_first(ny)}
    for i in far_first(ny):
        gy[i].start()
    copy(10, gy_send, gram_all.at[place], gy2_sem.at[0], sibling).start()

    for i in range(1, nx):
        there = sketch.at[lax.rem(x + nx - i, nx), other]
        copy(8, there, there, fwd_sem.at[i - 1], sibling).wait_recv()
    pairs = nz // 2
    for i in far_first(pairs) + [0]:
        to = lax.rem(z // 2 + i, pairs)
        at = pl.ds(pl.multiple_of(to * 2 * per_z, 2 * per_z), 2 * per_z)
        total = dot(tile_t[0, at, :], sketch[0].reshape(rows, size))
        for j in range(1, nx):
            total = total + dot(tile_t[j, at, :], sketch[j].reshape(rows, size))
        p_send[pl.ds(2 * to, 2)] = total.astype(BF16).reshape(2, per_z, size)
        targets = [2 * to, 2 * to + 1] if i else [z + 1 - 2 * lax.rem(z, 2)]
        for t in targets:
            slot = lax.rem(t + nz - z, nz) - 1
            copy(11, p_send.at[t], p_recv.at[slot], p_sem.at[0], (t * nx + x, c)).start()

    for i in near_first:
        gy[i].wait_recv()
        there = gram_all.at[half * ny + lax.rem(y + ny - i, ny)]
        copy(10, there, there, gy2_sem.at[0], sibling).start()
    copy(10, gram_all.at[other], gram_all.at[other], gy2_sem.at[0], sibling).wait_recv()
    work[:top, :top] = gram_all[:, 0].reshape(top, top)
    work[:top, top:size] = gram_all[:, 1].reshape(top, top)
    work[top:, :top] = jnp.zeros((top, top), F32)
    work[top:, top:size] = gram_all[:, 2].reshape(top, top)
    diagonal = lax.broadcasted_iota(jnp.int32, (size, size), 0)
    work[:, size:] = jnp.where(diagonal == lax.broadcasted_iota(jnp.int32, (size, size), 1), 1.0, 0.0)
    eliminate(work)

    product = p_send[z].astype(F32)
    copy(11, p_recv, p_recv, p_sem.at[0], sibling).wait_recv()
    for i in range(1, nz):
        product = product + p_recv[i - 1].astype(F32)
    inverse_high, inverse_low = split2(work[:, size:])
    product_high, product_low = split2(product)
    result = dot(
        jnp.concatenate([inverse_high, inverse_high, inverse_low], axis=1),
        jnp.concatenate([product_high, product_low, product_high], axis=1),
        ((1,), (1,)),
    )
    o_send[...] = result.reshape(o_send.shape)
    spot = pl.ds(pl.multiple_of(x * per_x + z * per_z, per_z), per_z)
    for i, j in around:
        target = at_zx(i, j)
        copy(12, o_send.at[target[0]], o_recv.at[:, spot], o_sem.at[0], target).start()
    o_recv[:, spot] = o_send[r]
    share = size // nc
    take = pl.ds(pl.multiple_of(c * share, share), share)
    share_high, share_low = split2(work[take, size:])
    held = sketch[x].reshape(rows, size)
    basis_ref[...] = dot(share_high, held, ((1,), (1,))) + dot(share_low, held, ((1,), (1,)))
    wait_sent(0, pair_send)
    wait_sent(1, rows_recv)
    wait_sent(2, rs_recv)
    wait_sent(3, rs_recv)
    wait_sent(4, rs_send)
    wait_sent(5, gx_recv)
    wait_sent(6, sketch.at[pl.ds(0, nx - 1), mine])
    wait_sent(7, gz_recv)
    wait_sent(8, sketch.at[pl.ds(0, nx - 1), mine])
    wait_sent(9, gram_all.at[pl.ds(0, ny - 1)])
    wait_sent(10, gram_all.at[mine])
    wait_sent(11, p_recv)
    others = o_send.at[pl.ds(0, len(around))]
    copy(12, others, others, o_sem.at[0], sibling).wait()
    out_ref[...] = o_recv[...]


def local(nx, nz, nc, row_features, col_features, test_block):
    rows, width = row_features.shape
    columns, size = test_block.shape
    per_x = columns // nx
    per_z = per_x // nz
    share = size // nc
    piece = rows // nc
    vmem = pltpu.VMEM

    def sems(count):
        return pltpu.SemaphoreType.DMA((count,))

    basis_t, projected = pl.pallas_call(
        functools.partial(kernel, nx, nz, nc),
        out_shape=(
            jax.ShapeDtypeStruct((share, rows), F32),
            jax.ShapeDtypeStruct((size // (nx * nz), columns), F32),
        ),
        in_specs=[pl.BlockSpec(memory_space=pl.ANY)] * 3,
        out_specs=(pl.BlockSpec(memory_space=vmem),) * 2,
        scratch_shapes=[
            vmem((width, rows), F32),
            vmem((width, columns), F32),
            vmem((columns, size), BF16),
            vmem((rows, 3 * width), BF16),
            vmem((per_x, 3 * width), BF16),
            vmem((rows, size), F32),
            vmem((rows // 2, size), BF16),
            vmem((rows // 2, size), BF16),
            vmem((nc // 2, piece, size), BF16),
            vmem((nc // 2 - 1, piece, size), BF16),
            vmem((nx - 1, width, rows), F32),
            vmem((piece, size), BF16),
            vmem((nx, nc, piece, size), BF16),
            vmem((nx, per_x, rows), BF16),
            vmem((nc, 3, size // 2 // nc, size // 2), F32),
            vmem((nx - 1, 3, size // 2 // nc, size // 2), F32),
            vmem((3, size // 2 // nc, size // 2), F32),
            vmem((nz - 1, 3, size // 2 // nc, size // 2), F32),
            vmem((3, size // 2 // nc, size // 2), F32),
            vmem((nc, 3, size // 2 // nc, size // 2), F32),
            vmem((nz, per_z, size), BF16),
            vmem((nz - 1, per_z, size), BF16),
            vmem((size, 2 * size), F32),
            vmem((nx * nz, size // (nx * nz), per_z), F32),
            vmem((size // (nx * nz), columns), F32),
            sems(1 + 2 * STEPS),
            sems(13),
            sems(nx - 1),
            sems(1),
            sems(1),
            sems(nc // 2 - 1),
            sems(1),
            sems(1),
            sems(nx - 1),
            sems(nx - 1),
            sems(1),
            sems(nc // 2 - 1),
            sems(1),
            sems(1),
            sems(1),
        ],
        compiler_params=pltpu.CompilerParams(
            collective_id=0, has_side_effects=True, vmem_limit_bytes=VMEM_LIMIT
        ),
    )(row_features.T, col_features.T, test_block)
    return basis_t.T, projected


def solution(mesh, nx=ALONG_X):
    nz, nc = mesh.shape["rows"] // nx, mesh.shape["cols"]
    return jax.shard_map(
        functools.partial(local, nx, nz, nc),
        mesh=mesh,
        in_specs=(P("rows", None), P("cols", None), P("cols", None)),
        out_specs=(P("rows", "cols"), P("rows", "cols")),
        check_vma=False,
    )
```

time: 71.8 us -> 63.4 us (0.88)
  Pallas kernels: 67.8 us -> 61.4 us
  local copies, waits for them, and re-layouts: 2.94 us -> 1.27 us
    pallas_call x1, Pallas kernels: 67.8 us -> 61.4 us  [local(): pl.pallas_call(functools.partial(kernel, nx, nz, nc), out_shape=(jax.Shap...]
    unnamed x2, local copies, waits for them, and re-layouts: 2.94 us -> 1.27 us
where the time goes in v2:
time: 63.4 us; the launch traced here: 63.3 us
  Pallas kernels  61.4 us (97%)
  local copies, waits for them, and re-layouts  1.27 us (2%)
  between operations  0.64 us (1%)
    pallas_call x1, Pallas kernels, local(): pl.pallas_call(functools.partial(kernel, nx, nz, nc), out_shape=(jax.Shap...  61.4 us
    unnamed x2, local copies, waits for them, and re-layouts  1.27 us

profile of v2, /device:TPU:1, one launch (start us, length us, event | category | flops | bytes accessed | tf_op | source)
XLA Modules:
  0.0 63.3 jit_solution(14619510988774236592)
XLA Ops:
  0.6 61.4 %shard_map.50 = (f32[16,512]{1,0:T(8,128)S(1)}, f32[8,4096]{1,0:T(8,128)S(1)}) custom-call(f32[64,512]{1,0:T(8,128)} %bitcast.5, f32[64,4096]{1,0:T(8,128)} %bitcast.4, bf16[4096,256]{1,0:T(8,128)(2,1)} %test_hbm.1), custom_call_target="tpu_custom_call" | custom-call | tf_op jit(solution)/shard_map/pallas_call | solution.py:334
  62.1 0.6 copy.7
  62.7 0.7 %copy.8 = f32[8,4096]{1,0:T(8,128)} copy(f32[8,4096]{1,0:T(8,128)S(1)} %get-tuple-element.9) | data formatting | bytes 262144

commit v3 on v2

--- a/solution.py
+++ b/solution.py
@@ -11,7 +11,8 @@
 MESH = pl.DeviceIdType.MESH
 F32, BF16 = jnp.float32, jnp.bfloat16
 ALONG_X = 4
-PANEL = 16
+PANEL = 32
+PART = 16
 STEPS = 2
 VMEM_LIMIT = 56_300_000
 
@@ -53,30 +54,44 @@
 
 def eliminate(work):
     n = work.shape[0]
-    row = lax.broadcasted_iota(jnp.int32, (PANEL, 1), 0)
-    for p in range(n // PANEL):
-        first = p * PANEL
+    row = lax.broadcasted_iota(jnp.int32, (8, 128), 0)
+    groups = PANEL // 8
+    for first in range(0, n, PANEL):
+        after = first + PANEL
         base = (first // 128) * 128
         offset = first - base
-        end = n + ((first + PANEL + 127) // 128) * 128
-        panel = work[first : first + PANEL, base:end]
-        tiles = panel.shape[1] // 128
-        column = [
-            jnp.broadcast_to(panel[:, offset + j : offset + j + 1], (PANEL, 128))
-            for j in range(PANEL)
+        end = n + ((after + 127) // 128) * 128
+        tiles = range(base, end, 128)
+        panel = [
+            [work[first + 8 * g : first + 8 * g + 8, t : t + 128] for t in tiles] for g in range(groups)
         ]
-        for k in range(PANEL):
-            inverse_root = lax.rsqrt(column[k][k : k + 1, :])
-            lower = column[k] * inverse_root
-            for j in range(k + 1, PANEL):
-                column[j] = column[j] - lower * lower[j : j + 1, :]
-            pivot_row = panel[k : k + 1, :] * jnp.concatenate([inverse_root] * tiles, axis=1)
-            below = jnp.concatenate([jnp.where(row > k, lower, 0.0)] * tiles, axis=1)
-            panel = jnp.where(
-                row == k, jnp.broadcast_to(pivot_row, panel.shape), panel - below * pivot_row
-            )
-        work[first : first + PANEL, base:end] = panel
-        after = first + PANEL
+        for part in range(0, PANEL, PART):
+            column = {
+                j: {
+                    g: jnp.broadcast_to(panel[g][0][:, offset + j : offset + j + 1], (8, 128))
+                    for g in range(j // 8, groups)
+                }
+                for j in range(part, part + PART)
+            }
+            for k in range(part, part + PART):
+                own, at = k // 8, k % 8
+                inverse_root = lax.rsqrt(column[k][own][at : at + 1, :])
+                lower = {g: v * inverse_root for g, v in column[k].items()}
+                for j in range(k + 1, part + PART):
+                    factor = lower[j // 8][j % 8 : j % 8 + 1, :]
+                    column[j] = {g: v - lower[g] * factor for g, v in column[j].items()}
+                below = jnp.where(row > at, lower[own], 0.0)
+                for t in range(len(tiles)):
+                    pivot_row = panel[own][t][at : at + 1, :] * inverse_root
+                    panel[own][t] = jnp.where(
+                        row == at,
+                        jnp.broadcast_to(pivot_row, (8, 128)),
+                        panel[own][t] - below * pivot_row,
+                    )
+                    for g in range(own + 1, groups):
+                        panel[g][t] = panel[g][t] - lower[g] * pivot_row
+        panel = jnp.concatenate([jnp.concatenate(g, axis=1) for g in panel], axis=0)
+        work[first:after, base:end] = panel
         if after < n:
             high, mid, low = split3(panel)
             start = (after // 128) * 128
@@ -93,14 +108,14 @@
     row_left, col_left, partial, pair_send, pair_recv, rs_send, rs_recv, rows_recv, own_sketch, sketch,
     tile_t, gram, gx_recv, gz_send, gz_recv, gy_send, gram_all,
     p_send, p_recv, work, o_send, o_recv,
-    in_sem, sent_sem, rows_sem, pair_sem, rs_sem, ag_sem, ag2_sem, gx_sem, xag_sem, fwd_sem, gz_sem, gy_sem, gy2_sem,
+    in_sem, sent_sem, far_sem, rows_sem, pair_sem, rs_sem, ag_sem, ag2_sem, gx_sem, xag_sem, fwd_sem, gz_sem, gy_sem, gy2_sem,
     p_sem, o_sem,
 ):
     r, c = lax.axis_index("rows"), lax.axis_index("cols")
     z, x = r // nx, lax.rem(r, nx)
     ny = nc // 2
     y, half = c // 2, lax.rem(c, 2)
-    rows, size = partial.shape
+    rows, size = 2 * partial.shape[0], partial.shape[1]
     piece = rows // nc
     width = row_ref.shape[0]
     scale = 1.0 / math.sqrt(width)
@@ -154,17 +169,23 @@
 
     loads[0].wait()
     row_left[...] = left_terms(row_ref[...], scale)
-    for n, at in enumerate(steps):
-        loads[2 * n + 1].wait()
-        tile = cubed(dot(row_left[...], right_terms(col_ref[:, at], 1.0)))
-        loads[2 * n + 2].wait()
-        share = dot(tile, test_ref[at, :])
-        partial[...] = partial[...] + share if n else share
-
     def half_of(which):
         return pl.ds(pl.multiple_of(which * (rows // 2), rows // 2), rows // 2)
 
-    pair_send[...] = partial[half_of(1 - half), :].astype(BF16)
+    def partial_sketch(which, loading):
+        left = row_left[half_of(which), :]
+        total = None
+        for n, at in enumerate(steps):
+            if loading:
+                loads[2 * n + 1].wait()
+            tile = cubed(dot(left, right_terms(col_ref[:, at], 1.0)))
+            if loading:
+                loads[2 * n + 2].wait()
+            share = dot(tile, test_ref[at, :])
+            total = share if total is None else total + share
+        return total
+
+    pair_send[...] = partial_sketch(1 - half, True).astype(BF16)
     pl.semaphore_wait(barrier, ny + len(around))
 
     pair = copy(0, pair_send, pair_recv, pair_sem.at[0], sibling)
@@ -172,15 +193,16 @@
     feat = [copy(1, row_ref, rows_recv.at[i - 1], rows_sem.at[i - 1], at_x(i)) for i in range(1, nx)]
     for one in feat:
         one.start()
+    partial[...] = partial_sketch(half, False)
     pair.wait_recv()
-    partial[half_of(half), :] += pair_recv[...].astype(F32)
-    rs_send[...] = partial[half_of(half), :].astype(BF16).reshape(rs_send.shape)
+    partial[...] += pair_recv[...].astype(F32)
+    rs_send[...] = partial[...].astype(BF16).reshape(rs_send.shape)
     rs = [copy(2, rs_send.at[lax.rem(y + i, ny)], rs_recv.at[i - 1], rs_sem.at[0], at_y(i)) for i in far_first(ny)]
     for one in rs:
         one.start()
     own = pl.ds(pl.multiple_of(x * per_x, per_x), per_x)
     col_left[...] = left_terms(col_ref[:, own], 1.0)
-    total = partial[pl.ds(pl.multiple_of(place * piece, piece), piece), :]
+    total = partial[pl.ds(pl.multiple_of(y * piece, piece), piece), :]
     copy(2, rs_recv, rs_recv, rs_sem.at[0], sibling).wait_recv()
     for i in range(1, ny):
         total = total + rs_recv[i - 1].astype(F32)
@@ -191,6 +213,8 @@
     for i in far_first(ny):
         ag[i].start()
     copy(4, own_sketch, sketch.at[x, place], ag2_sem.at[0], sibling).start()
+    opposite = nx // 2
+    copy(13, own_sketch, sketch.at[x, place], far_sem.at[0], at_x(opposite)).start()
 
     block = min(256, per_x)
     for i in range(nx):
@@ -204,6 +228,11 @@
         def _(m):
             at = pl.ds(pl.multiple_of(m * block, block), block)
             tile_t[at_block, at, :] = cubed(dot(col_left[at, :], right))
+
+    far = lax.rem(x + opposite, nx)
+    copy(13, own_sketch, sketch.at[far, place], far_sem.at[0], sibling).wait_recv()
+    for i in far_first(ny):
+        copy(14, sketch.at[far, place], sketch.at[far, place], far_sem.at[1], at_y(i)).start()
 
     near_first = far_first(ny)[::-1]
     for i in near_first:
@@ -224,9 +253,10 @@
     gx = [copy(5, gram.at[place], gx_recv.at[i - 1], gx_sem.at[0], at_x(i)) for i in range(1, nx)]
     for one in gx:
         one.start()
-    xag = [copy(6, sketch.at[x, mine], sketch.at[x, mine], xag_sem.at[i - 1], at_x(i)) for i in range(1, nx)]
-    for one in xag:
-        one.start()
+    beside = [i for i in range(1, nx) if i != opposite]
+    xag = {i: copy(6, sketch.at[x, mine], sketch.at[x, mine], xag_sem.at[i - 1], at_x(i)) for i in beside}
+    for i in beside:
+        xag[i].start()
     slice_sum = gram[place]
     copy(5, gx_recv, gx_recv, gx_sem.at[0], sibling).wait_recv()
     for i in range(1, nx):
@@ -236,24 +266,16 @@
     for one in gz:
         one.start()
 
-    for i in range(1, nx):
-        xag[i - 1].wait_recv()
+    copy(14, rs_recv, rs_recv, far_sem.at[1], sibling).wait_recv()
+    copy(8, sketch.at[far, mine], sketch.at[far, mine], fwd_sem.at[opposite - 1], sibling).start()
+    for i in beside:
+        xag[i].wait_recv()
         there = sketch.at[lax.rem(x + nx - i, nx), mine]
         copy(8, there, there, fwd_sem.at[i - 1], sibling).start()
-
-    copy(7, gz_recv, gz_recv, gz_sem.at[0], sibling).wait_recv()
-    for i in range(1, nz):
-        slice_sum = slice_sum + gz_recv[i - 1]
-    gy_send[...] = slice_sum
-    gram_all[place] = slice_sum
-    gy = {i: copy(9, gy_send, gram_all.at[place], gy_sem.at[i - 1], at_y(i)) for i in far_first(ny)}
-    for i in far_first(ny):
-        gy[i].start()
-    copy(10, gy_send, gram_all.at[place], gy2_sem.at[0], sibling).start()
-
     for i in range(1, nx):
         there = sketch.at[lax.rem(x + nx - i, nx), other]
         copy(8, there, there, fwd_sem.at[i - 1], sibling).wait_recv()
+
     pairs = nz // 2
     for i in far_first(pairs) + [0]:
         to = lax.rem(z // 2 + i, pairs)
@@ -267,6 +289,16 @@
             slot = lax.rem(t + nz - z, nz) - 1
             copy(11, p_send.at[t], p_recv.at[slot], p_sem.at[0], (t * nx + x, c)).start()
 
+    copy(7, gz_recv, gz_recv, gz_sem.at[0], sibling).wait_recv()
+    for i in range(1, nz):
+        slice_sum = slice_sum + gz_recv[i - 1]
+    gy_send[...] = slice_sum
+    gram_all[place] = slice_sum
+    gy = {i: copy(9, gy_send, gram_all.at[place], gy_sem.at[i - 1], at_y(i)) for i in far_first(ny)}
+    for i in far_first(ny):
+        gy[i].start()
+    copy(10, gy_send, gram_all.at[place], gy2_sem.at[0], sibling).start()
+
     for i in near_first:
         gy[i].wait_recv()
         there = gram_all.at[half * ny + lax.rem(y + ny - i, ny)]
@@ -291,12 +323,12 @@
         jnp.concatenate([product_high, product_low, product_high], axis=1),
         ((1,), (1,)),
     )
-    o_send[...] = result.reshape(o_send.shape)
-    spot = pl.ds(pl.multiple_of(x * per_x + z * per_z, per_z), per_z)
+    o_send[...] = result.astype(BF16).reshape(o_send.shape)
+    spot = x * nz + z
     for i, j in around:
         target = at_zx(i, j)
-        copy(12, o_send.at[target[0]], o_recv.at[:, spot], o_sem.at[0], target).start()
-    o_recv[:, spot] = o_send[r]
+        copy(12, o_send.at[target[0]], o_recv.at[spot], o_sem.at[0], target).start()
+    o_recv[spot] = o_send[r]
     share = size // nc
     take = pl.ds(pl.multiple_of(c * share, share), share)
     share_high, share_low = split2(work[take, size:])
@@ -308,15 +340,19 @@
     wait_sent(3, rs_recv)
     wait_sent(4, rs_send)
     wait_sent(5, gx_recv)
-    wait_sent(6, sketch.at[pl.ds(0, nx - 1), mine])
+    if beside:
+        wait_sent(6, sketch.at[pl.ds(0, len(beside)), mine])
     wait_sent(7, gz_recv)
     wait_sent(8, sketch.at[pl.ds(0, nx - 1), mine])
     wait_sent(9, gram_all.at[pl.ds(0, ny - 1)])
     wait_sent(10, gram_all.at[mine])
     wait_sent(11, p_recv)
+    wait_sent(13, own_sketch)
+    wait_sent(14, rs_recv)
     others = o_send.at[pl.ds(0, len(around))]
     copy(12, others, others, o_sem.at[0], sibling).wait()
-    out_ref[...] = o_recv[...]
+    for k in range(nx * nz):
+        out_ref[:, k * per_z : (k + 1) * per_z] = o_recv[k].astype(F32)
 
 
 def local(nx, nz, nc, row_features, col_features, test_block):
@@ -345,7 +381,7 @@
             vmem((columns, size), BF16),
             vmem((rows, 3 * width), BF16),
             vmem((per_x, 3 * width), BF16),
-            vmem((rows, size), F32),
+            vmem((rows // 2, size), F32),
             vmem((rows // 2, size), BF16),
             vmem((rows // 2, size), BF16),
             vmem((nc // 2, piece, size), BF16),
@@ -363,10 +399,11 @@
             vmem((nz, per_z, size), BF16),
             vmem((nz - 1, per_z, size), BF16),
             vmem((size, 2 * size), F32),
-            vmem((nx * nz, size // (nx * nz), per_z), F32),
-            vmem((size // (nx * nz), columns), F32),
+            vmem((nx * nz, size // (nx * nz), per_z), BF16),
+            vmem((nx * nz, size // (nx * nz), per_z), BF16),
             sems(1 + 2 * STEPS),
-            sems(13),
+            sems(15),
+            sems(2),
             sems(nx - 1),
             sems(1),
             sems(1),

time: 63.4 us -> 59 us (0.931)
  Pallas kernels: 61.4 us -> 57 us
    pallas_call x1, Pallas kernels: 61.4 us -> 57 us  [local(): pl.pallas_call(functools.partial(kernel, nx, nz, nc), out_shape=(jax.Shap...]
where the time goes in v3:
time: 59 us; the launch traced here: 58.9 us
  Pallas kernels  57 us (97%)
  local copies, waits for them, and re-layouts  1.27 us (2%)
  between operations  0.64 us (1%)
    pallas_call x1, Pallas kernels, local(): pl.pallas_call(functools.partial(kernel, nx, nz, nc), out_shape=(jax.Shap...  57 us
    unnamed x2, local copies, waits for them, and re-layouts  1.27 us

profile of v3, /device:TPU:1, one launch (start us, length us, event | category | flops | bytes accessed | tf_op | source)
XLA Modules:
  0.0 58.9 jit_solution(10652933090861748052)
XLA Ops:
  0.6 57.0 %shard_map.50 = (f32[16,512]{1,0:T(8,128)S(1)}, f32[8,4096]{1,0:T(8,128)S(1)}) custom-call(f32[64,512]{1,0:T(8,128)} %bitcast.5, f32[64,4096]{1,0:T(8,128)} %bitcast.4, bf16[4096,256]{1,0:T(8,128)(2,1)} %test_hbm.1), custom_call_target="tpu_custom_call" | custom-call | tf_op jit(solution)/shard_map/pallas_call | solution.py:370
  57.6 0.6 %copy.7 = f32[512,16]{0,1:T(8,128)} copy(f32[512,16]{0,1:T(8,128)S(1)} %bitcast.3) | data formatting | bytes 65536
  58.2 0.7 %copy.8 = f32[8,4096]{1,0:T(8,128)} copy(f32[8,4096]{1,0:T(8,128)S(1)} %get-tuple-element.9) | data formatting | bytes 262144

commit v4 on v3

--- a/solution.py
+++ b/solution.py
@@ -13,6 +13,7 @@
 ALONG_X = 4
 PANEL = 32
 PART = 16
+ANTIPODE = 4
 STEPS = 2
 VMEM_LIMIT = 56_300_000
 
@@ -107,7 +108,7 @@
     row_ref, col_ref, test_ref,
     row_left, col_left, partial, pair_send, pair_recv, rs_send, rs_recv, rows_recv, own_sketch, sketch,
     tile_t, gram, gx_recv, gz_send, gz_recv, gy_send, gram_all,
-    p_send, p_recv, work, o_send, o_recv,
+    p_send, p_recv, relay_recv, work, o_send, o_recv,
     in_sem, sent_sem, far_sem, rows_sem, pair_sem, rs_sem, ag_sem, ag2_sem, gx_sem, xag_sem, fwd_sem, gz_sem, gy_sem, gy2_sem,
     p_sem, o_sem,
 ):
@@ -161,31 +162,35 @@
     for one in loads:
         one.start()
     barrier = pltpu.get_barrier_semaphore()
-    pl.semaphore_signal(barrier, inc=1, device_id=sibling, device_id_type=MESH)
+    for i, j in around:
+        pl.semaphore_signal(barrier, inc=1, device_id=at_zx(i, j), device_id_type=MESH)
     for i in far_first(ny):
         pl.semaphore_signal(barrier, inc=1, device_id=at_y(i), device_id_type=MESH)
-    for i, j in around:
-        pl.semaphore_signal(barrier, inc=1, device_id=at_zx(i, j), device_id_type=MESH)
+    pl.semaphore_signal(barrier, inc=1, device_id=sibling, device_id_type=MESH)
 
     loads[0].wait()
     row_left[...] = left_terms(row_ref[...], scale)
     def half_of(which):
         return pl.ds(pl.multiple_of(which * (rows // 2), rows // 2), rows // 2)
 
-    def partial_sketch(which, loading):
+    def partial_sketch(which, n, loading):
         left = row_left[half_of(which), :]
-        total = None
-        for n, at in enumerate(steps):
-            if loading:
-                loads[2 * n + 1].wait()
-            tile = cubed(dot(left, right_terms(col_ref[:, at], 1.0)))
-            if loading:
-                loads[2 * n + 2].wait()
-            share = dot(tile, test_ref[at, :])
-            total = share if total is None else total + share
-        return total
-
-    pair_send[...] = partial_sketch(1 - half, True).astype(BF16)
+        at = steps[n]
+        if loading:
+            loads[2 * n + 1].wait()
+        tile = cubed(dot(left, right_terms(col_ref[:, at], 1.0)))
+        if loading:
+            loads[2 * n + 2].wait()
+        return dot(tile, test_ref[at, :])
+
+    theirs = partial_sketch(1 - half, 0, True)
+    for n in range(1, STEPS):
+        theirs = theirs + partial_sketch(1 - half, n, True)
+    pair_send[...] = theirs.astype(BF16)
+    ours = partial_sketch(half, 0, False)
+    for n in range(1, STEPS // 2):
+        ours = ours + partial_sketch(half, n, False)
+    partial[...] = ours
     pl.semaphore_wait(barrier, ny + len(around))
 
     pair = copy(0, pair_send, pair_recv, pair_sem.at[0], sibling)
@@ -193,7 +198,8 @@
     feat = [copy(1, row_ref, rows_recv.at[i - 1], rows_sem.at[i - 1], at_x(i)) for i in range(1, nx)]
     for one in feat:
         one.start()
-    partial[...] = partial_sketch(half, False)
+    for n in range(STEPS // 2, STEPS):
+        partial[...] += partial_sketch(half, n, False)
     pair.wait_recv()
     partial[...] += pair_recv[...].astype(F32)
     rs_send[...] = partial[...].astype(BF16).reshape(rs_send.shape)
@@ -277,17 +283,29 @@
         copy(8, there, there, fwd_sem.at[i - 1], sibling).wait_recv()
 
     pairs = nz // 2
-    for i in far_first(pairs) + [0]:
+
+    def form(i):
         to = lax.rem(z // 2 + i, pairs)
         at = pl.ds(pl.multiple_of(to * 2 * per_z, 2 * per_z), 2 * per_z)
         total = dot(tile_t[0, at, :], sketch[0].reshape(rows, size))
         for j in range(1, nx):
             total = total + dot(tile_t[j, at, :], sketch[j].reshape(rows, size))
         p_send[pl.ds(2 * to, 2)] = total.astype(BF16).reshape(2, per_z, size)
-        targets = [2 * to, 2 * to + 1] if i else [z + 1 - 2 * lax.rem(z, 2)]
-        for t in targets:
-            slot = lax.rem(t + nz - z, nz) - 1
-            copy(11, p_send.at[t], p_recv.at[slot], p_sem.at[0], (t * nx + x, c)).start()
+
+    def send(*distances):
+        for d in distances:
+            slot = d - 1 if d < ANTIPODE or nz <= ANTIPODE else d - 2
+            copy(11, p_send.at[lax.rem(z + d, nz)], p_recv.at[slot], p_sem.at[0], at_z(d)).start()
+
+    relayed = nz == 2 * ANTIPODE
+    if relayed:
+        form(2)
+        relay = copy(15, p_send.at[lax.rem(z + ANTIPODE, nz)], relay_recv, p_sem.at[1], at_z(nz - 1))
+        relay.start()
+        form(3)
+        send(6)
+        form(1)
+        send(3, 2)
 
     copy(7, gz_recv, gz_recv, gz_sem.at[0], sibling).wait_recv()
     for i in range(1, nz):
@@ -299,10 +317,23 @@
         gy[i].start()
     copy(10, gy_send, gram_all.at[place], gy2_sem.at[0], sibling).start()
 
+    if relayed:
+        form(0)
+        send(7, 1)
+    else:
+        for i in range(pairs):
+            form(i)
+        send(*far_first(nz))
+
     for i in near_first:
         gy[i].wait_recv()
         there = gram_all.at[half * ny + lax.rem(y + ny - i, ny)]
         copy(10, there, there, gy2_sem.at[0], sibling).start()
+    if relayed:
+        relay.wait_recv()
+        joint = lax.rem(z + 5, nz)
+        p_send[joint] = (p_send[joint].astype(F32) + relay_recv[...].astype(F32)).astype(BF16)
+        send(5)
     copy(10, gram_all.at[other], gram_all.at[other], gy2_sem.at[0], sibling).wait_recv()
     work[:top, :top] = gram_all[:, 0].reshape(top, top)
     work[:top, top:size] = gram_all[:, 1].reshape(top, top)
@@ -314,8 +345,8 @@
 
     product = p_send[z].astype(F32)
     copy(11, p_recv, p_recv, p_sem.at[0], sibling).wait_recv()
-    for i in range(1, nz):
-        product = product + p_recv[i - 1].astype(F32)
+    for i in range(p_recv.shape[0]):
+        product = product + p_recv[i].astype(F32)
     inverse_high, inverse_low = split2(work[:, size:])
     product_high, product_low = split2(product)
     result = dot(
@@ -349,6 +380,8 @@
     wait_sent(11, p_recv)
     wait_sent(13, own_sketch)
     wait_sent(14, rs_recv)
+    if relayed:
+        wait_sent(15, relay_recv)
     others = o_send.at[pl.ds(0, len(around))]
     copy(12, others, others, o_sem.at[0], sibling).wait()
     for k in range(nx * nz):
@@ -397,12 +430,13 @@
             vmem((3, size // 2 // nc, size // 2), F32),
             vmem((nc, 3, size // 2 // nc, size // 2), F32),
             vmem((nz, per_z, size), BF16),
-            vmem((nz - 1, per_z, size), BF16),
+            vmem((nz - 2 if nz == 2 * ANTIPODE else nz - 1, per_z, size), BF16),
+            vmem((per_z, size), BF16),
             vmem((size, 2 * size), F32),
             vmem((nx * nz, size // (nx * nz), per_z), BF16),
             vmem((nx * nz, size // (nx * nz), per_z), BF16),
             sems(1 + 2 * STEPS),
-            sems(15),
+            sems(16),
             sems(2),
             sems(nx - 1),
             sems(1),
@@ -415,7 +449,7 @@
             sems(1),
             sems(nc // 2 - 1),
             sems(1),
-            sems(1),
+            sems(2),
             sems(1),
         ],
         compiler_params=pltpu.CompilerParams(

time: 59 us -> 58.2 us (0.986)
  Pallas kernels: 57 us -> 56.2 us
    pallas_call x1, Pallas kernels: 57 us -> 56.2 us  [local(): pl.pallas_call(functools.partial(kernel, nx, nz, nc), out_shape=(jax.Shap...]
where the time goes in v4:
time: 58.2 us; the launch traced here: 58.1 us
  Pallas kernels  56.2 us (97%)
  local copies, waits for them, and re-layouts  1.27 us (2%)
  between operations  0.64 us (1%)
    pallas_call x1, Pallas kernels, local(): pl.pallas_call(functools.partial(kernel, nx, nz, nc), out_shape=(jax.Shap...  56.2 us
    unnamed x2, local copies, waits for them, and re-layouts  1.27 us

profile of v4, /device:TPU:1, one launch (start us, length us, event | category | flops | bytes accessed | tf_op | source)
XLA Modules:
  0.0 58.1 jit_solution(14137993100691963969)
XLA Ops:
  0.6 56.2 %shard_map.50 = (f32[16,512]{1,0:T(8,128)S(1)}, f32[8,4096]{1,0:T(8,128)S(1)}) custom-call(f32[64,512]{1,0:T(8,128)} %bitcast.5, f32[64,4096]{1,0:T(8,128)} %bitcast.4, bf16[4096,256]{1,0:T(8,128)(2,1)} %test_hbm.1), custom_call_target="tpu_custom_call" | custom-call | tf_op jit(solution)/shard_map/pallas_call | solution.py:403
  56.8 0.6 %copy.7 = f32[512,16]{0,1:T(8,128)} copy(f32[512,16]{0,1:T(8,128)S(1)} %bitcast.3) | data formatting | bytes 65536
  57.4 0.7 %copy.8 = f32[8,4096]{1,0:T(8,128)} copy(f32[8,4096]{1,0:T(8,128)S(1)} %get-tuple-element.9) | data formatting | bytes 262144

commit v5 on v4

--- a/solution.py
+++ b/solution.py
@@ -15,7 +15,7 @@
 PART = 16
 ANTIPODE = 4
 STEPS = 2
-VMEM_LIMIT = 56_300_000
+VMEM_LIMIT = 56_400_000
 
 
 def far_first(length):
@@ -384,8 +384,19 @@
         wait_sent(15, relay_recv)
     others = o_send.at[pl.ds(0, len(around))]
     copy(12, others, others, o_sem.at[0], sibling).wait()
-    for k in range(nx * nz):
-        out_ref[:, k * per_z : (k + 1) * per_z] = o_recv[k].astype(F32)
+    out_ref[...] = o_recv[...]
+
+
+def finish(basis_ref, pieces_ref, basis_hbm, out_hbm, out_ref, sem):
+    basis = pltpu.make_async_copy(basis_ref, basis_hbm, sem.at[0])
+    basis.start()
+    width = pieces_ref.shape[2]
+    for k in range(pieces_ref.shape[0]):
+        out_ref[:, k * width : (k + 1) * width] = pieces_ref[k].astype(F32)
+    out = pltpu.make_async_copy(out_ref, out_hbm, sem.at[1])
+    out.start()
+    basis.wait()
+    out.wait()
 
 
 def local(nx, nz, nc, row_features, col_features, test_block):
@@ -400,11 +411,11 @@
     def sems(count):
         return pltpu.SemaphoreType.DMA((count,))
 
-    basis_t, projected = pl.pallas_call(
+    basis_t, pieces = pl.pallas_call(
         functools.partial(kernel, nx, nz, nc),
         out_shape=(
             jax.ShapeDtypeStruct((share, rows), F32),
-            jax.ShapeDtypeStruct((size // (nx * nz), columns), F32),
+            jax.ShapeDtypeStruct((nx * nz, size // (nx * nz), per_z), BF16),
         ),
         in_specs=[pl.BlockSpec(memory_space=pl.ANY)] * 3,
         out_specs=(pl.BlockSpec(memory_space=vmem),) * 2,
@@ -456,6 +467,17 @@
             collective_id=0, has_side_effects=True, vmem_limit_bytes=VMEM_LIMIT
         ),
     )(row_features.T, col_features.T, test_block)
+    basis_t, projected = pl.pallas_call(
+        finish,
+        out_shape=(
+            jax.ShapeDtypeStruct((share, rows), F32),
+            jax.ShapeDtypeStruct((size // (nx * nz), columns), F32),
+        ),
+        in_specs=[pl.BlockSpec(memory_space=vmem)] * 2,
+        out_specs=(pl.BlockSpec(memory_space=pl.ANY),) * 2,
+        scratch_shapes=[vmem((size // (nx * nz), columns), F32), sems(2)],
+        compiler_params=pltpu.CompilerParams(vmem_limit_bytes=2 * 1024 * 1024),
+    )(basis_t, pieces)
     return basis_t.T, projected
 
 

time: 58.2 us -> 57.6 us (0.990)
  local copies, waits for them, and re-layouts: 1.27 us -> 0 us
  Pallas kernels: 56.2 us -> 56.9 us
    unnamed x2 -> x0, local copies, waits for them, and re-layouts: 1.27 us -> none
    pallas_call x0 -> x1, Pallas kernels: none -> 0.69 us  [local(): pl.pallas_call(finish, out_shape=(jax.ShapeDtypeStruct((share, rows), F32...]
where the time goes in v5:
time: 57.6 us; the launch traced here: 57.5 us
  Pallas kernels  56.9 us (99%)
  between operations  0.64 us (1%)
    pallas_call x1, Pallas kernels, local(): pl.pallas_call(functools.partial(kernel, nx, nz, nc), out_shape=(jax.Shap...  56.2 us

profile of v5, /device:TPU:1, one launch (start us, length us, event | category | flops | bytes accessed | tf_op | source)
XLA Modules:
  0.0 57.5 jit_solution(5381035269733413503)
XLA Ops:
  0.6 56.2 %shard_map.50 = (f32[16,512]{1,0:T(8,128)S(1)}, bf16[32,8,128]{2,1,0:T(8,128)(2,1)S(1)}) custom-call(f32[64,512]{1,0:T(8,128)} %bitcast.4, f32[64,4096]{1,0:T(8,128)} %bitcast.3, bf16[4096,256]{1,0:T(8,128)(2,1)} %test_hbm.1), custom_call_target="tpu_custom_call" | custom-call | tf_op jit(solution)/shard_map/pallas_call | solution.py:414
  56.8 0.7 %shard_map.51 = (f32[16,512]{1,0:T(8,128)}, f32[8,4096]{1,0:T(8,128)}) custom-call(f32[16,512]{1,0:T(8,128)S(1)} %get-tuple-element.6.basis_ref, bf16[32,8,128]{2,1,0:T(8,128)(2,1)S(1)} %get-tuple-element.7.pieces_ref), custom_call_target="tpu_custom_call" | custom-call | tf_op jit(solution)/shard_map/pallas_call | solution.py:470
